TPU v7x, 32 devices: a whole 2x2x4 slice. The times are simulated.
32 devices in a mesh: dp: 8 (over y, x, core), mp: 4 (over z).
Axes of the slice: x: 2, y: 2, z: 4, core: 2. Of those that a mesh axis runs over, the one named last changes fastest.
Arguments:
- hidden_in: bfloat16 [2, 32, 4096], P(None, 'dp', 'mp'), may hold values from -6 to 6
- rec_gain: float32 [2, 4096], replicated, may hold values from 0.5 to 1.5
- rec_in_x: bfloat16 [2, 4096, 4096], P(None, 'dp', 'mp'), may hold values from -0.09375 to 0.09375
- rec_in_y: bfloat16 [2, 4096, 4096], P(None, 'dp', 'mp'), may hold values from -0.09375 to 0.09375
- conv_weight: float32 [2, 4, 4096], P(None, None, 'mp'), may hold values from -3 to 3
- conv_bias: float32 [2, 4096], P(None, 'mp'), may hold values from -3 to 3
- gate_x_weight: bfloat16 [2, 16, 256, 256], P(None, 'mp'), may hold values from -0.375 to 0.375
- gate_x_bias: float32 [2, 4096], P(None, 'mp'), may hold values from -4 to 4
- gate_a_weight: bfloat16 [2, 16, 256, 256], P(None, 'mp'), may hold values from -0.375 to 0.375
- gate_a_bias: float32 [2, 4096], P(None, 'mp'), may hold values from -4 to 4
- decay_param: float32 [2, 4096], P(None, 'mp'), may hold values from -9 to -1
- rec_out: bfloat16 [2, 4096, 4096], P(None, 'dp', 'mp'), may hold values from -0.09375 to 0.09375
- lru_state: bfloat16 [2, 32, 4096], P(None, 'dp', 'mp'), may hold values from -6 to 6
- conv_state: bfloat16 [2, 3, 32, 4096], P(None, None, 'dp', 'mp'), may hold values from -6 to 6
- scale_index: int32 [2], replicated, may hold values from 0 to 7
- attn_gain: float32 [4096], replicated, may hold values from 0.5 to 1.5
- attn_q: bfloat16 [4096, 4096], P('dp', 'mp'), may hold values from -0.09375 to 0.09375
- attn_kv: bfloat16 [4096, 512], P('dp', 'mp'), may hold values from -0.09375 to 0.09375
- attn_out: bfloat16 [4096, 4096], P('dp', 'mp'), may hold values from -0.09375 to 0.09375
- key_cache: bfloat16 [32, 2048, 256], P('dp', 'mp'), may hold values from -400 to 400
- value_cache: bfloat16 [32, 2048, 256], P('dp', 'mp'), may hold values from -6 to 6
- positions: int32 [32], P('dp'), may hold values from 1 to 6143
Outputs:
- hidden_out: bfloat16 [2, 32, 4096], P(None, 'dp', 'mp')
- lru_out: bfloat16 [2, 32, 4096], P(None, 'dp', 'mp')
- conv_out: bfloat16 [2, 3, 32, 4096], P(None, None, 'dp', 'mp')
- new_kv: bfloat16 [2, 32, 512], P(None, 'dp', 'mp')
Inputs may be any that keep to these rules, and one draw needn't show every extreme that they name: `positions`: the count of tokens a sequence has seen; the cache holds its last min(that count, 2048) tokens.
All inputs are finite; a program needn't handle non-finite values.
Results may differ from a plain program's by a relative error of at most 0.03.
Values may be sent and summed in bfloat16 or wider, within the bound.
A program may use at most 64 MiB of HBM per device.

v0:
```python
import jax
import jax.numpy as jnp
from jax import lax
from jax.sharding import PartitionSpec as P

HEADS = 16
HEAD_DIM = 256
WIN = 2048
LAYERS = 2
STEPS = 2


def joined(array, axis, join):
    gathered = jax.tree.map(
        lambda a, kind: lax.all_gather(a.astype(kind), axis),
        array,
        (jnp.bfloat16, jnp.bfloat16, jnp.bfloat16),
    )

    def take(source):
        return jax.tree.map(
            lambda a, own: lax.dynamic_index_in_dim(a, source, 0, False).astype(own.dtype),
            gathered,
            array,
        )

    return lax.fori_loop(
        1, lax.axis_size(axis), lambda source, state: join(state, take(source)), take(0)
    )


def norm_rows(values, gain):
    mean_sq = jnp.mean(values * values, axis=-1, keepdims=True)
    return (values * lax.rsqrt(mean_sq + 1e-06) * gain).astype(jnp.bfloat16)


def spread_project(normed, weight):
    spread = lax.all_to_all(normed, "dp", split_axis=1, concat_axis=0, tiled=True)
    return lax.psum_scatter(
        jnp.dot(spread, weight, preferred_element_type=jnp.float32),
        "dp",
        scatter_dimension=0,
        tiled=True,
    )


def full_stream(stream):
    return lax.all_gather(stream, "mp", axis=1, tiled=True)


def full_features(values):
    return lax.all_gather(values, "mp", axis=1, tiled=True)


def lru_gate(filtered_half, weight, bias):
    rows = filtered_half.shape[0]
    shaped = filtered_half.reshape(rows, weight.shape[0], weight.shape[1])
    mixed = jnp.einsum("bhi,hij->bhj", shaped, weight, preferred_element_type=jnp.float32)
    return jax.nn.sigmoid(mixed.reshape(rows, -1) + bias)


def combine(first, second):
    top_first, total_first, summed_first = first
    top_second, total_second, summed_second = second
    best = jnp.maximum(top_first, top_second)
    fade_first = jnp.exp(top_first - best)
    fade_second = jnp.exp(top_second - best)
    total = total_first * fade_first + total_second * fade_second
    summed = summed_first * fade_first[..., None] + summed_second * fade_second[..., None]
    return (best, total, summed)


def recurrent_layer(
    stream,
    gain,
    in_x,
    in_y,
    conv_taps,
    conv_shift,
    gx_weight,
    gx_bias,
    ga_weight,
    ga_bias,
    decay,
    out_weight,
    state,
    window,
):
    normed = norm_rows(full_stream(stream), gain)
    width = in_x.shape[1]
    both = spread_project(normed, jnp.concatenate([in_x, in_y], axis=1))
    branch_input = both[:, :width]
    branch_gate = both[:, width:]
    driven = branch_input.astype(jnp.bfloat16)
    gating = jax.nn.gelu(branch_gate, approximate=True)
    taps = jnp.concatenate([window, driven[None]], 0)
    filtered = jnp.sum(taps.astype(jnp.float32) * conv_taps[:, None, :], axis=0) + conv_shift
    filtered_half = filtered.astype(jnp.bfloat16)
    input_gate = lru_gate(filtered_half, gx_weight, gx_bias)
    decay_gate = lru_gate(filtered_half, ga_weight, ga_bias)
    log_decay = -8.0 * decay_gate * jax.nn.softplus(decay)
    state = jnp.exp(log_decay) * state + jnp.sqrt(1.0 - jnp.exp(2.0 * log_decay)) * (
        input_gate * filtered
    )
    mixed = (state * gating).astype(jnp.bfloat16)
    stream = stream + spread_project(full_features(mixed), out_weight)
    return (stream, state, taps[1:])


def attention_layer(
    stream,
    gain,
    w_query,
    w_keyvalue,
    w_out,
    key_cache,
    value_cache,
    positions,
    fresh_keys,
    fresh_values,
    step,
):
    normed = norm_rows(full_stream(stream), gain)
    query_cols = w_query.shape[1]
    local = spread_project(normed, jnp.concatenate([w_query, w_keyvalue], axis=1)).astype(
        jnp.bfloat16
    )
    kv_local = local[:, query_cols:]
    rows = local.shape[0]
    groups = full_features(local).reshape(rows, -1, local.shape[1])
    query = groups[:, :, :query_cols].reshape(rows, HEADS, HEAD_DIM)
    key_value = groups[:, :, query_cols:].reshape(rows, 2 * HEAD_DIM)
    fresh_keys.append(key_value[:, :HEAD_DIM])
    fresh_values.append(key_value[:, HEAD_DIM:])
    slots = key_cache.shape[1]
    slot_ids = lax.axis_index("mp") * slots + jnp.arange(slots, dtype=jnp.int32)
    position = positions[:, None]
    held = position - 1 - jnp.mod(position - 1 - slot_ids[None, :], WIN)
    valid = ((held >= 0) & (held >= position + step - WIN + 1))[:, None, :]
    scores = jnp.einsum(
        "bhd,bsd->bhs", query, key_cache, preferred_element_type=jnp.float32
    ) * HEAD_DIM ** (-0.5)
    masked = jnp.where(valid, scores, -1e30)
    top = jnp.max(masked, axis=-1)
    weights = jnp.where(valid, jnp.exp(masked - top[..., None]), 0.0)
    total = jnp.sum(weights, axis=-1)
    summed = jnp.einsum(
        "bhs,bsd->bhd",
        weights.astype(jnp.bfloat16),
        value_cache,
        preferred_element_type=jnp.float32,
    )
    top, total, summed = joined((top, total, summed), "mp", combine)
    new_keys = jnp.stack(fresh_keys, 1)
    new_values = jnp.stack(fresh_values, 1)
    fresh_scores = jnp.einsum(
        "bhd,bnd->bhn", query, new_keys, preferred_element_type=jnp.float32
    ) * HEAD_DIM ** (-0.5)
    best = jnp.maximum(top, jnp.max(fresh_scores, axis=-1))
    fade = jnp.exp(top - best)
    fresh_weights = jnp.exp(fresh_scores - best[..., None])
    total = total * fade + jnp.sum(fresh_weights, axis=-1)
    summed = summed * fade[..., None] + jnp.einsum(
        "bhn,bnd->bhd",
        fresh_weights.astype(jnp.bfloat16),
        new_values,
        preferred_element_type=jnp.float32,
    )
    attended = (summed / total[..., None]).astype(jnp.bfloat16).reshape(rows, HEADS * HEAD_DIM)
    stream = stream + spread_project(attended, w_out)
    return (stream, kv_local)


def body(
    hidden_in,
    rec_gain,
    rec_in_x,
    rec_in_y,
    conv_weight,
    conv_bias,
    gate_x_weight,
    gate_x_bias,
    gate_a_weight,
    gate_a_bias,
    decay_param,
    rec_out,
    lru_state,
    conv_state,
    scale_index,
    attn_gain,
    attn_q,
    attn_kv,
    attn_out,
    key_cache,
    value_cache,
    positions,
):
    scales = 2.0 ** ((scale_index.astype(jnp.float32) - 4.0) * 0.5)
    states = [lru_state[layer].astype(jnp.float32) * scales[layer] for layer in range(LAYERS)]
    windows = [conv_state[layer] for layer in range(LAYERS)]
    fresh_keys = []
    fresh_values = []
    outputs = []
    kv_parts = []
    for step in range(STEPS):
        stream = hidden_in[step].astype(jnp.float32)
        for layer in range(LAYERS):
            stream, states[layer], windows[layer] = recurrent_layer(
                stream,
                rec_gain[layer],
                rec_in_x[layer],
                rec_in_y[layer],
                conv_weight[layer],
                conv_bias[layer],
                gate_x_weight[layer],
                gate_x_bias[layer],
                gate_a_weight[layer],
                gate_a_bias[layer],
                decay_param[layer],
                rec_out[layer],
                states[layer],
                windows[layer],
            )
        stream, kv_local = attention_layer(
            stream,
            attn_gain,
            attn_q,
            attn_kv,
            attn_out,
            key_cache,
            value_cache,
            positions,
            fresh_keys,
            fresh_values,
            step,
        )
        kv_parts.append(kv_local)
        outputs.append(stream.astype(jnp.bfloat16))
    lru_new = jnp.stack(
        [(states[layer] / scales[layer]).astype(jnp.bfloat16) for layer in range(LAYERS)], 0
    )
    return (jnp.stack(outputs, 0), lru_new, jnp.stack(windows, 0), jnp.stack(kv_parts, 0))


def solution(mesh):
    placed = (
        P(None, "dp", "mp"),
        P(),
        P(None, "dp", "mp"),
        P(None, "dp", "mp"),
        P(None, None, "mp"),
        P(None, "mp"),
        P(None, "mp", None, None),
        P(None, "mp"),
        P(None, "mp", None, None),
        P(None, "mp"),
        P(None, "mp"),
        P(None, "dp", "mp"),
        P(None, "dp", "mp"),
        P(None, None, "dp", "mp"),
        P(),
        P(),
        P("dp", "mp"),
        P("dp", "mp"),
        P("dp", "mp"),
        P("dp", "mp", None),
        P("dp", "mp", None),
        P("dp"),
    )
    return jax.shard_map(
        body,
        mesh=mesh,
        in_specs=placed,
        out_specs=(
            P(None, "dp", "mp"),
            P(None, "dp", "mp"),
            P(None, None, "dp", "mp"),
            P(None, "dp", "mp"),
        ),
        check_vma=False,
    )
```

profile of v0, /device:TPU:0, one launch (start us, length us, event | category | flops | bytes accessed | tf_op | source)
XLA Modules:
  0.0 668.5 jit_solution(16265052284147277069)
XLA Ops:
  8.0 14.9 %all-gather.4 = f32[1,4,4096]{2,1,0:T(4,128)S(1)} all-gather(f32[1,4,1024]{2,1,0:T(4,128)S(1)} %get-tuple-element.445), channel_id=6, replica_groups=mesh['dp'=8,'mp'=4] {'mp'}, dimensions={2}, use_global_device_ids=true | all-gather | bytes 81920 | tf_op jit(solution)/shard_map/all_gather | solution.py:48
  23.1 13.3 %all-gather = f32[1,4,4096]{2,1,0:T(4,128)S(1)} all-gather(f32[1,4,1024]{2,1,0:T(4,128)S(1)} %get-tuple-element.444), channel_id=2, replica_groups=mesh['dp'=8,'mp'=4] {'mp'}, dimensions={2}, use_global_device_ids=true | all-gather | bytes 81920 | tf_op jit(solution)/shard_map/all_gather | solution.py:48
  65.6 52.1 %all-reduce.33.cloned.1.call-done = (f32[32,2048]{1,0:T(8,128)}, f32[32,2048]{1,0:T(8,128)}) async-done(((f32[32,2048]{1,0:T(8,128)}, f32[32,2048]{1,0:T(8,128)}), (f32[32,2048]{1,0:T(8,128)}, f32[32,2048]{1,0:T(8,128)})) %all-reduce.33.cloned.1.call-update) | async-done | bytes 524304
  126.6 13.8 %all_gather.75 = bf16[4,4096]{1,0:T(4,128)(2,1)} all-gather(bf16[4,1024]{1,0:T(4,128)(2,1)S(1)} %fusion.125), channel_id=1, replica_groups=mesh['dp'=8,'mp'=4] {'mp'}, dimensions={1}, use_global_device_ids=true | all-gather | bytes 40960 | tf_op jit(solution)/shard_map/all_gather | solution.py:52
  143.8 13.8 %all_gather.65 = bf16[4,4096]{1,0:T(4,128)(2,1)} all-gather(bf16[4,1024]{1,0:T(4,128)(2,1)S(1)} %get-tuple-element.424), channel_id=1, replica_groups=mesh['dp'=8,'mp'=4] {'mp'}, dimensions={1}, use_global_device_ids=true | all-gather | bytes 40960 | tf_op jit(solution)/shard_map/all_gather | solution.py:52
  169.2 52.6 %all-reduce.31.cloned.1.call-done = (f32[32,1024]{1,0:T(8,128)}, f32[32,1024]{1,0:T(8,128)}) async-done(((f32[32,1024]{1,0:T(8,128)}, f32[32,1024]{1,0:T(8,128)}), (f32[32,1024]{1,0:T(8,128)}, f32[32,1024]{1,0:T(8,128)})) %all-reduce.31.cloned.1.call-update) | async-done | bytes 262160
  222.6 13.2 %all_gather.76 = f32[4,4096]{1,0:T(4,128)S(1)} all-gather(f32[4,1024]{1,0:T(4,128)S(1)} %get-tuple-element.441), channel_id=1, replica_groups=mesh['dp'=8,'mp'=4] {'mp'}, dimensions={1}, use_global_device_ids=true | all-gather | bytes 81920 | tf_op jit(solution)/shard_map/all_gather | solution.py:48
  235.9 13.2 %all_gather.66 = f32[4,4096]{1,0:T(4,128)S(1)} all-gather(f32[4,1024]{1,0:T(4,128)S(1)} %get-tuple-element.440), channel_id=1, replica_groups=mesh['dp'=8,'mp'=4] {'mp'}, dimensions={1}, use_global_device_ids=true | all-gather | bytes 81920 | tf_op jit(solution)/shard_map/all_gather | solution.py:48
  272.2 52.5 %all-reduce.29.cloned.1.call-done = (f32[32,2048]{1,0:T(8,128)}, f32[32,2048]{1,0:T(8,128)}) async-done(((f32[32,2048]{1,0:T(8,128)}, f32[32,2048]{1,0:T(8,128)}), (f32[32,2048]{1,0:T(8,128)}, f32[32,2048]{1,0:T(8,128)})) %all-reduce.29.cloned.1.call-update) | async-done | bytes 524304
  331.6 13.9 %all_gather.77 = bf16[4,4096]{1,0:T(4,128)(2,1)} all-gather(bf16[4,1024]{1,0:T(4,128)(2,1)S(1)} %fusion.124), channel_id=1, replica_groups=mesh['dp'=8,'mp'=4] {'mp'}, dimensions={1}, use_global_device_ids=true | all-gather | bytes 40960 | tf_op jit(solution)/shard_map/all_gather | solution.py:52
  349.5 13.9 %all_gather.67 = bf16[4,4096]{1,0:T(4,128)(2,1)} all-gather(bf16[4,1024]{1,0:T(4,128)(2,1)S(1)} %get-tuple-element.422), channel_id=1, replica_groups=mesh['dp'=8,'mp'=4] {'mp'}, dimensions={1}, use_global_device_ids=true | all-gather | bytes 40960 | tf_op jit(solution)/shard_map/all_gather | solution.py:52
  375.2 52.5 %all-reduce.27.cloned.1.call-done = (f32[32,1024]{1,0:T(8,128)}, f32[32,1024]{1,0:T(8,128)}) async-done(((f32[32,1024]{1,0:T(8,128)}, f32[32,1024]{1,0:T(8,128)}), (f32[32,1024]{1,0:T(8,128)}, f32[32,1024]{1,0:T(8,128)})) %all-reduce.27.cloned.1.call-update) | async-done | bytes 262160
  428.5 13.2 %all_gather.68 = f32[4,4096]{1,0:T(4,128)S(1)} all-gather(f32[4,1024]{1,0:T(4,128)S(1)} %dynamic-slice_add_fusion.4), channel_id=1, replica_groups=mesh['dp'=8,'mp'=4] {'mp'}, dimensions={1}, use_global_device_ids=true | all-gather | bytes 81920 | tf_op jit(solution)/shard_map/all_gather | solution.py:48
  442.7 13.2 %all_gather.78 = f32[4,4096]{1,0:T(4,128)S(1)} all-gather(f32[4,1024]{1,0:T(4,128)S(1)} %dynamic-slice_add_fusion.1), channel_id=1, replica_groups=mesh['dp'=8,'mp'=4] {'mp'}, dimensions={1}, use_global_device_ids=true | all-gather | bytes 81920 | tf_op jit(solution)/shard_map/all_gather | solution.py:48
  473.9 25.9 %all-reduce.34 = (bf16[32,1152]{1,0:T(8,128)(2,1)S(1)}, bf16[32,1152]{1,0:T(8,128)(2,1)S(1)}) all-reduce(f32[32,1152]{1,0:T(8,128)} %fusion.177, f32[32,1152]{1,0:T(8,128)S(1)} %fusion.175), channel_id=20, replica_groups=mesh['dp'=8,'mp'=4] {'dp'}, use_global_device_ids=true, to_apply=%region_24.25.clone | all-reduce | flops 73728 | bytes 442368
  499.8 13.2 %all_gather.69 = bf16[4,4608]{1,0:T(4,128)(2,1)S(1)} all-gather(bf16[4,1152]{1,0:T(4,128)(2,1)S(1)} %dynamic-slice_convert_fusion.1), channel_id=1, replica_groups=mesh['dp'=8,'mp'=4] {'mp'}, dimensions={1}, use_global_device_ids=true | all-gather | bytes 46080 | tf_op jit(solution)/shard_map/all_gather | solution.py:52
  513.1 13.2 %all_gather.79 = bf16[4,4608]{1,0:T(4,128)(2,1)S(1)} all-gather(bf16[4,1152]{1,0:T(4,128)(2,1)S(1)} %dynamic-slice_convert_fusion), channel_id=1, replica_groups=mesh['dp'=8,'mp'=4] {'mp'}, dimensions={1}, use_global_device_ids=true | all-gather | bytes 46080 | tf_op jit(solution)/shard_map/all_gather | solution.py:52
  528.5 13.4 %all-gather.3 = bf16[16,16,256]{2,1,0:T(8,128)(2,1)S(1)} all-gather(bf16[4,16,256]{2,1,0:T(8,128)(2,1)S(1)} %convolution_convert_fusion.1), channel_id=5, replica_groups=mesh['dp'=8,'mp'=4] {'mp'}, dimensions={0}, use_global_device_ids=true | all-gather | bytes 163840 | tf_op jit(solution)/shard_map/all_gather | solution.py:15
  541.9 10.8 %all-gather.9 = bf16[4,4,16]{2,1,0:T(4,128)(2,1)S(1)} all-gather(bf16[1,4,16]{2,1,0:T(4,128)(2,1)S(1)} %bitcast.382), channel_id=4, replica_groups=mesh['dp'=8,'mp'=4] {'mp'}, dimensions={0}, use_global_device_ids=true | all-gather | bytes 640 | tf_op jit(solution)/shard_map/all_gather | solution.py:15
  552.7 7.6 %all-gather.8 = bf16[4,4,16]{2,1,0:T(4,128)(2,1)S(1)} all-gather(bf16[1,4,16]{2,1,0:T(4,128)(2,1)S(1)} %convert_bitcast_fusion.3), channel_id=3, replica_groups=mesh['dp'=8,'mp'=4] {'mp'}, dimensions={0}, use_global_device_ids=true | all-gather | bytes 640 | tf_op jit(solution)/shard_map/all_gather | solution.py:15
  564.8 13.4 %all-gather.7 = bf16[16,16,256]{2,1,0:T(8,128)(2,1)S(1)} all-gather(bf16[4,16,256]{2,1,0:T(8,128)(2,1)S(1)} %convolution_convert_fusion), channel_id=9, replica_groups=mesh['dp'=8,'mp'=4] {'mp'}, dimensions={0}, use_global_device_ids=true | all-gather | bytes 163840 | tf_op jit(solution)/shard_map/all_gather | solution.py:15
  578.2 9.6 %all-gather.11 = bf16[4,4,16]{2,1,0:T(4,128)(2,1)S(1)} all-gather(bf16[1,4,16]{2,1,0:T(4,128)(2,1)S(1)} %bitcast.381), channel_id=8, replica_groups=mesh['dp'=8,'mp'=4] {'mp'}, dimensions={0}, use_global_device_ids=true | all-gather | bytes 640 | tf_op jit(solution)/shard_map/all_gather | solution.py:15
  587.8 7.6 %all-gather.10 = bf16[4,4,16]{2,1,0:T(4,128)(2,1)S(1)} all-gather(bf16[1,4,16]{2,1,0:T(4,128)(2,1)S(1)} %convert_bitcast_fusion.1), channel_id=7, replica_groups=mesh['dp'=8,'mp'=4] {'mp'}, dimensions={0}, use_global_device_ids=true | all-gather | bytes 640 | tf_op jit(solution)/shard_map/all_gather | solution.py:15
  608.5 51.3 %all-reduce.25.cloned.1.call-done = (f32[32,1024]{1,0:T(8,128)}, f32[32,1024]{1,0:T(8,128)}) async-done(((f32[32,1024]{1,0:T(8,128)}, f32[32,1024]{1,0:T(8,128)}), (f32[32,1024]{1,0:T(8,128)}, f32[32,1024]{1,0:T(8,128)})) %all-reduce.25.cloned.1.call-update) | async-done | bytes 262160
  (245 shorter events, 142.1 us)
Async XLA Ops:
  7.2 519.2 %copy-start = (bf16[4,512,256]{2,1,0:T(8,128)(2,1)S(1)}, bf16[4,512,256]{2,1,0:T(8,128)(2,1)}, u32[]{:S(2)}) copy-start(bf16[4,512,256]{2,1,0:T(8,128)(2,1)} %param.45) | copy-start | bytes 3145732
  38.1 14.1 %all-to-all-start = ((bf16[4,8,512]{2,0,1:T(4,128)(2,1)}), bf16[4,8,512]{2,0,1:T(4,128)(2,1)S(1)}, u32[]{:S(2)}, u32[]{:S(2)}) async-start(bf16[4,8,512]{2,0,1:T(4,128)(2,1)} %bitcast.12), calls=%async_computation | async-start | bytes 65536 | tf_op jit(solution)/shard_map/all_to_all | solution.py:38
  44.6 81.1 %copy-start.14 = (f32[1,1024]{1,0:T(1,128)}, f32[1,1024]{1,0:T(1,128)S(1)}, u32[]{:S(2)}) copy-start(f32[1,1024]{1,0:T(1,128)S(1)} %get-tuple-element.453) | copy-start | bytes 12292
  52.2 9.0 %all-to-all-start.6 = ((bf16[4,8,512]{2,0,1:T(4,128)(2,1)}), bf16[4,8,512]{2,0,1:T(4,128)(2,1)S(1)}, u32[]{:S(2)}, u32[]{:S(2)}) async-start(bf16[4,8,512]{2,0,1:T(4,128)(2,1)} %bitcast.72), calls=%async_computation.6 | async-start | bytes 65536 | tf_op jit(solution)/shard_map/all_to_all | solution.py:38
  56.4 61.3 %all-reduce.33.cloned.1.call-start = ((), (), s32[]{:S(2)}) async-start(), calls=%async_computation.16 | async-start | bytes 1048576
  63.6 103.0 %copy-start.1 = (bf16[2,512,1024]{2,1,0:T(8,128)(2,1)S(1)}, bf16[2,512,1024]{2,1,0:T(8,128)(2,1)}, u32[]{:S(2)}) copy-start(bf16[2,512,1024]{2,1,0:T(8,128)(2,1)} %param.37) | copy-start | bytes 6291460
  121.8 100.0 %copy-start.9 = (bf16[2,4,1024]{2,1,0:T(4,128)(2,1)S(1)}, bf16[2,4,1024]{2,1,0:T(4,128)(2,1)}, u32[]{:S(2)}) copy-start(bf16[2,4,1024]{2,1,0:T(4,128)(2,1)} %param.26) | copy-start | bytes 49156
  140.4 17.2 %all-to-all-start.7 = ((bf16[4,8,512]{2,0,1:T(4,128)(2,1)}), bf16[4,8,512]{2,0,1:T(4,128)(2,1)S(1)}, u32[]{:S(2)}, u32[]{:S(2)}) async-start(bf16[4,8,512]{2,0,1:T(4,128)(2,1)} %bitcast.80), calls=%async_computation.7 | async-start | bytes 65536 | tf_op jit(solution)/shard_map/all_to_all | solution.py:38
  157.6 9.0 %all-to-all-start.1 = ((bf16[4,8,512]{2,0,1:T(4,128)(2,1)}), bf16[4,8,512]{2,0,1:T(4,128)(2,1)S(1)}, u32[]{:S(2)}, u32[]{:S(2)}) async-start(bf16[4,8,512]{2,0,1:T(4,128)(2,1)} %bitcast.31), calls=%async_computation.1 | async-start | bytes 65536 | tf_op jit(solution)/shard_map/all_to_all | solution.py:38
  161.8 60.0 %all-reduce.31.cloned.1.call-start = ((), (), s32[]{:S(2)}) async-start(), calls=%async_computation.15 | async-start | bytes 524288
  168.5 98.4 %copy-start.5 = (bf16[512,1024]{1,0:T(8,128)(2,1)S(1)}, bf16[512,1024]{1,0:T(8,128)(2,1)}, u32[]{:S(2)}) copy-start(bf16[512,1024]{1,0:T(8,128)(2,1)} %get-tuple-element.428) | copy-start | bytes 3145732
  250.0 8.1 %all-to-all-start.2 = ((bf16[4,8,512]{2,0,1:T(4,128)(2,1)}), bf16[4,8,512]{2,0,1:T(4,128)(2,1)S(1)}, u32[]{:S(2)}, u32[]{:S(2)}) async-start(bf16[4,8,512]{2,0,1:T(4,128)(2,1)} %bitcast.36), calls=%async_computation.2 | async-start | bytes 65536 | tf_op jit(solution)/shard_map/all_to_all | solution.py:38
  258.1 8.1 %all-to-all-start.8 = ((bf16[4,8,512]{2,0,1:T(4,128)(2,1)}), bf16[4,8,512]{2,0,1:T(4,128)(2,1)S(1)}, u32[]{:S(2)}, u32[]{:S(2)}) async-start(bf16[4,8,512]{2,0,1:T(4,128)(2,1)} %bitcast.82), calls=%async_computation.8 | async-start | bytes 65536 | tf_op jit(solution)/shard_map/all_to_all | solution.py:38
  261.4 63.2 %all-reduce.29.cloned.1.call-start = ((), (), s32[]{:S(2)}) async-start(), calls=%async_computation.14 | async-start | bytes 1048576
  329.1 126.9 %copy-start.25 = (f32[4096]{0:T(1024)S(1)}, f32[4096]{0:T(1024)}, u32[]{:S(2)}) copy-start(f32[4096]{0:T(1024)} %param.41) | copy-start | bytes 49156
  345.4 18.0 %all-to-all-start.9 = ((bf16[4,8,512]{2,0,1:T(4,128)(2,1)}), bf16[4,8,512]{2,0,1:T(4,128)(2,1)S(1)}, u32[]{:S(2)}, u32[]{:S(2)}) async-start(bf16[4,8,512]{2,0,1:T(4,128)(2,1)} %bitcast.90), calls=%async_computation.9 | async-start | bytes 65536 | tf_op jit(solution)/shard_map/all_to_all | solution.py:38
  363.4 9.0 %all-to-all-start.3 = ((bf16[4,8,512]{2,0,1:T(4,128)(2,1)}), bf16[4,8,512]{2,0,1:T(4,128)(2,1)S(1)}, u32[]{:S(2)}, u32[]{:S(2)}) async-start(bf16[4,8,512]{2,0,1:T(4,128)(2,1)} %bitcast.55), calls=%async_computation.3 | async-start | bytes 65536 | tf_op jit(solution)/shard_map/all_to_all | solution.py:38
  367.5 60.3 %all-reduce.27.cloned.1.call-start = ((), (), s32[]{:S(2)}) async-start(), calls=%async_computation.13 | async-start | bytes 524288
  442.7 83.7 %copy-start.23 = (pred[4,512]{1,0:T(4,128)(4,1)S(1)}, pred[4,512]{1,0:T(4,128)(4,1)}, u32[]{:S(2)}) copy-start(pred[4,512]{1,0:T(4,128)(4,1)} %get-tuple-element.463) | copy-start | bytes 6148
  456.7 8.1 %all-to-all-start.4 = ((bf16[4,8,512]{2,0,1:T(4,128)(2,1)}), bf16[4,8,512]{2,0,1:T(4,128)(2,1)S(1)}, u32[]{:S(2)}, u32[]{:S(2)}) async-start(bf16[4,8,512]{2,0,1:T(4,128)(2,1)} %bitcast.58), calls=%async_computation.4 | async-start | bytes 65536 | tf_op jit(solution)/shard_map/all_to_all | solution.py:38
  464.8 8.1 %all-to-all-start.10 = ((bf16[4,8,512]{2,0,1:T(4,128)(2,1)}), bf16[4,8,512]{2,0,1:T(4,128)(2,1)S(1)}, u32[]{:S(2)}, u32[]{:S(2)}) async-start(bf16[4,8,512]{2,0,1:T(4,128)(2,1)} %bitcast.92), calls=%async_computation.10 | async-start | bytes 65536 | tf_op jit(solution)/shard_map/all_to_all | solution.py:38
  561.4 35.4 %all-to-all-start.5 = ((bf16[4,8,512]{2,0,1:T(4,128)(2,1)}), bf16[4,8,512]{2,0,1:T(4,128)(2,1)S(1)}, u32[]{:S(2)}, u32[]{:S(2)}) async-start(bf16[4,8,512]{2,0,1:T(4,128)(2,1)} %copy.95), calls=%async_computation.5 | async-start | bytes 65536 | tf_op jit(solution)/shard_map/all_to_all | solution.py:38
  596.9 9.1 %all-to-all-start.11 = ((bf16[4,8,512]{2,0,1:T(4,128)(2,1)}), bf16[4,8,512]{2,0,1:T(4,128)(2,1)S(1)}, u32[]{:S(2)}, u32[]{:S(2)}) async-start(bf16[4,8,512]{2,0,1:T(4,128)(2,1)} %copy.107), calls=%async_computation.11 | async-start | bytes 65536 | tf_op jit(solution)/shard_map/all_to_all | solution.py:38
  601.1 58.7 %all-reduce.25.cloned.1.call-start = ((), (), s32[]{:S(2)}) async-start(), calls=%async_computation.12 | async-start | bytes 524288
  (23 other events, 882.1 us)
Sparse Core Ops, SparseCore 0:
  63.7 53.8 all-reduce.32
  168.6 53.0 all-reduce.30
  270.8 53.8 all-reduce.28
  374.7 53.0 all-reduce.26
  608.0 51.7 all-reduce.24
where the time goes:
time: 671 us; the launch traced here: 669 us
  waiting for transfers between devices  293 us (44%)
  blocking collectives  251 us (37%)
  starting transfers between devices  43.8 us (7%)
  matrix products  25.1 us (4%)
  other arithmetic  20.7 us (3%)
  local copies, waits for them, and re-layouts  20 us (3%)
  between operations  15.2 us (2%)
    unnamed x10, waiting for transfers between devices  261 us
    all_gather x6, blocking collectives, full_features(): return lax.all_gather(values, 'mp', axis=1, tiled=True)  81.7 us
    all_gather x6, blocking collectives, full_stream(): return lax.all_gather(stream, 'mp', axis=1, tiled=True)  81 us
    all_gather x6, blocking collectives, joined(): lax.all_gather(a.astype(kind), axis)  62.3 us
    all_to_all x12, starting transfers between devices, spread_project(): lax.all_to_all(normed, 'dp', split_axis=1, concat_axis=0, tiled=True)  43.7 us
    all_to_all x12, waiting for transfers between devices, spread_project(): lax.all_to_all(normed, 'dp', split_axis=1, concat_axis=0, tiled=True)  31.4 us
    unnamed x1, blocking collectives  25.9 us
    dot_general x12, matrix products, spread_project(): jnp.dot(spread, weight, preferred_element_type=jnp.float32)  15.4 us
  transfers between devices with their start and end apart: 17, of which 13 were waited for; matrix products, arithmetic and copies ran while one was open for 3% of the time, Pallas kernels for 0%

commit v1 on v0

--- a/solution.py
+++ b/solution.py
@@ -35,7 +35,9 @@
 
 
 def spread_project(normed, weight):
-    spread = lax.all_to_all(normed, "dp", split_axis=1, concat_axis=0, tiled=True)
+    cells = jnp.split(normed, lax.axis_size("dp"), axis=1)
+    received = lax.all_to_all(jnp.stack(cells), "dp", 0, 0)
+    spread = jnp.concatenate(received, axis=0)
     return lax.psum_scatter(
         jnp.dot(spread, weight, preferred_element_type=jnp.float32),
         "dp",

time: 671 us -> 713 us (1.063)
  local copies, waits for them, and re-layouts: 20 us -> 75.4 us
  waiting for transfers between devices: 293 us -> 280 us
    unnamed x66 -> x142, local copies, waits for them, and re-layouts: 2.03 us -> 52 us
    all_to_all x12, waiting for transfers between devices: 31.4 us -> 20.1 us  [spread_project(): received = lax.all_to_all(jnp.stack(cells), 'dp', 0, 0)]
  transfers between devices with their start and end apart: 17 -> 17, of which waited for: 13 -> 11; matrix products, arithmetic and copies ran while one was open for 3% -> 8% of each run, Pallas kernels for 0% -> 0%
where the time goes in v1:
time: 713 us; the launch traced here: 710 us
  waiting for transfers between devices  280 us (39%)
  blocking collectives  248 us (35%)
  local copies, waits for them, and re-layouts  75.4 us (11%)
  starting transfers between devices  45.4 us (6%)
  matrix products  26.6 us (4%)
  other arithmetic  19.4 us (3%)
  between operations  15.1 us (2%)
    unnamed x10, waiting for transfers between devices  260 us
    all_gather x6, blocking collectives, full_stream(): return lax.all_gather(stream, 'mp', axis=1, tiled=True)  81 us
    all_gather x6, blocking collectives, full_features(): return lax.all_gather(values, 'mp', axis=1, tiled=True)  78.8 us
    all_gather x6, blocking collectives, joined(): lax.all_gather(a.astype(kind), axis)  62.3 us
    unnamed x142, local copies, waits for them, and re-layouts  52 us
    all_to_all x12, starting transfers between devices, spread_project(): received = lax.all_to_all(jnp.stack(cells), 'dp', 0, 0)  45.3 us
    unnamed x1, blocking collectives  25.9 us
    all_to_all x12, waiting for transfers between devices, spread_project(): received = lax.all_to_all(jnp.stack(cells), 'dp', 0, 0)  20.1 us
  transfers between devices with their start and end apart: 17, of which 11 were waited for; matrix products, arithmetic and copies ran while one was open for 8% of the time, Pallas kernels for 0%

profile of v1, /device:TPU:0, one launch (start us, length us, event | category | flops | bytes accessed | tf_op | source)
XLA Modules:
  0.0 710.2 jit_solution(11852351363770767202)
XLA Ops:
  8.0 14.9 %all-gather.4 = f32[1,4,4096]{2,1,0:T(4,128)S(1)} all-gather(f32[1,4,1024]{2,1,0:T(4,128)S(1)} %get-tuple-element.445), channel_id=6, replica_groups=mesh['dp'=8,'mp'=4] {'mp'}, dimensions={2}, use_global_device_ids=true | all-gather | bytes 81920 | tf_op jit(solution)/shard_map/all_gather | solution.py:50
  23.1 13.3 %all-gather = f32[1,4,4096]{2,1,0:T(4,128)S(1)} all-gather(f32[1,4,1024]{2,1,0:T(4,128)S(1)} %get-tuple-element.444), channel_id=2, replica_groups=mesh['dp'=8,'mp'=4] {'mp'}, dimensions={2}, use_global_device_ids=true | all-gather | bytes 81920 | tf_op jit(solution)/shard_map/all_gather | solution.py:50
  74.8 52.2 %all-reduce.33.cloned.1.call-done = (f32[32,2048]{1,0:T(8,128)}, f32[32,2048]{1,0:T(8,128)}) async-done(((f32[32,2048]{1,0:T(8,128)}, f32[32,2048]{1,0:T(8,128)}), (f32[32,2048]{1,0:T(8,128)}, f32[32,2048]{1,0:T(8,128)})) %all-reduce.33.cloned.1.call-update) | async-done | bytes 524304
  135.0 13.1 %all_gather.65 = bf16[4,4096]{1,0:T(4,128)(2,1)S(1)} all-gather(bf16[4,1024]{1,0:T(4,128)(2,1)S(1)} %get-tuple-element.424), channel_id=1, replica_groups=mesh['dp'=8,'mp'=4] {'mp'}, dimensions={1}, use_global_device_ids=true | all-gather | bytes 40960 | tf_op jit(solution)/shard_map/all_gather | solution.py:54
  157.2 13.1 %all_gather.75 = bf16[4,4096]{1,0:T(4,128)(2,1)S(1)} all-gather(bf16[4,1024]{1,0:T(4,128)(2,1)S(1)} %fusion.127), channel_id=1, replica_groups=mesh['dp'=8,'mp'=4] {'mp'}, dimensions={1}, use_global_device_ids=true | all-gather | bytes 40960 | tf_op jit(solution)/shard_map/all_gather | solution.py:54
  187.3 51.2 %all-reduce.31.cloned.1.call-done = (f32[32,1024]{1,0:T(8,128)}, f32[32,1024]{1,0:T(8,128)}) async-done(((f32[32,1024]{1,0:T(8,128)}, f32[32,1024]{1,0:T(8,128)}), (f32[32,1024]{1,0:T(8,128)}, f32[32,1024]{1,0:T(8,128)})) %all-reduce.31.cloned.1.call-update) | async-done | bytes 262160
  239.3 13.2 %all_gather.76 = f32[4,4096]{1,0:T(4,128)S(1)} all-gather(f32[4,1024]{1,0:T(4,128)S(1)} %get-tuple-element.441), channel_id=1, replica_groups=mesh['dp'=8,'mp'=4] {'mp'}, dimensions={1}, use_global_device_ids=true | all-gather | bytes 81920 | tf_op jit(solution)/shard_map/all_gather | solution.py:50
  252.7 13.2 %all_gather.66 = f32[4,4096]{1,0:T(4,128)S(1)} all-gather(f32[4,1024]{1,0:T(4,128)S(1)} %get-tuple-element.440), channel_id=1, replica_groups=mesh['dp'=8,'mp'=4] {'mp'}, dimensions={1}, use_global_device_ids=true | all-gather | bytes 81920 | tf_op jit(solution)/shard_map/all_gather | solution.py:50
  292.8 53.1 %all-reduce.29.cloned.1.call-done = (f32[32,2048]{1,0:T(8,128)}, f32[32,2048]{1,0:T(8,128)}) async-done(((f32[32,2048]{1,0:T(8,128)}, f32[32,2048]{1,0:T(8,128)}), (f32[32,2048]{1,0:T(8,128)}, f32[32,2048]{1,0:T(8,128)})) %all-reduce.29.cloned.1.call-update) | async-done | bytes 524304
  351.9 13.1 %all_gather.67 = bf16[4,4096]{1,0:T(4,128)(2,1)S(1)} all-gather(bf16[4,1024]{1,0:T(4,128)(2,1)S(1)} %get-tuple-element.422), channel_id=1, replica_groups=mesh['dp'=8,'mp'=4] {'mp'}, dimensions={1}, use_global_device_ids=true | all-gather | bytes 40960 | tf_op jit(solution)/shard_map/all_gather | solution.py:54
  374.0 13.1 %all_gather.77 = bf16[4,4096]{1,0:T(4,128)(2,1)S(1)} all-gather(bf16[4,1024]{1,0:T(4,128)(2,1)S(1)} %fusion.126), channel_id=1, replica_groups=mesh['dp'=8,'mp'=4] {'mp'}, dimensions={1}, use_global_device_ids=true | all-gather | bytes 40960 | tf_op jit(solution)/shard_map/all_gather | solution.py:54
  405.2 52.0 %all-reduce.27.cloned.1.call-done = (f32[32,1024]{1,0:T(8,128)}, f32[32,1024]{1,0:T(8,128)}) async-done(((f32[32,1024]{1,0:T(8,128)}, f32[32,1024]{1,0:T(8,128)}), (f32[32,1024]{1,0:T(8,128)}, f32[32,1024]{1,0:T(8,128)})) %all-reduce.27.cloned.1.call-update) | async-done | bytes 262160
  457.9 13.2 %all_gather.68 = f32[4,4096]{1,0:T(4,128)S(1)} all-gather(f32[4,1024]{1,0:T(4,128)S(1)} %dynamic-slice_add_fusion.4), channel_id=1, replica_groups=mesh['dp'=8,'mp'=4] {'mp'}, dimensions={1}, use_global_device_ids=true | all-gather | bytes 81920 | tf_op jit(solution)/shard_map/all_gather | solution.py:50
  472.0 13.2 %all_gather.78 = f32[4,4096]{1,0:T(4,128)S(1)} all-gather(f32[4,1024]{1,0:T(4,128)S(1)} %dynamic-slice_add_fusion.1), channel_id=1, replica_groups=mesh['dp'=8,'mp'=4] {'mp'}, dimensions={1}, use_global_device_ids=true | all-gather | bytes 81920 | tf_op jit(solution)/shard_map/all_gather | solution.py:50
  508.3 25.9 %all-reduce.34 = (bf16[32,1152]{1,0:T(8,128)(2,1)S(1)}, bf16[32,1152]{1,0:T(8,128)(2,1)S(1)}) all-reduce(f32[32,1152]{1,0:T(8,128)} %fusion.179, f32[32,1152]{1,0:T(8,128)S(1)} %fusion.177), channel_id=20, replica_groups=mesh['dp'=8,'mp'=4] {'dp'}, use_global_device_ids=true, to_apply=%region_24.25.clone | all-reduce | flops 73728 | bytes 442368
  534.2 13.2 %all_gather.69 = bf16[4,4608]{1,0:T(4,128)(2,1)S(1)} all-gather(bf16[4,1152]{1,0:T(4,128)(2,1)S(1)} %dynamic-slice_convert_fusion.1), channel_id=1, replica_groups=mesh['dp'=8,'mp'=4] {'mp'}, dimensions={1}, use_global_device_ids=true | all-gather | bytes 46080 | tf_op jit(solution)/shard_map/all_gather | solution.py:54
  547.4 13.2 %all_gather.79 = bf16[4,4608]{1,0:T(4,128)(2,1)S(1)} all-gather(bf16[4,1152]{1,0:T(4,128)(2,1)S(1)} %dynamic-slice_convert_fusion), channel_id=1, replica_groups=mesh['dp'=8,'mp'=4] {'mp'}, dimensions={1}, use_global_device_ids=true | all-gather | bytes 46080 | tf_op jit(solution)/shard_map/all_gather | solution.py:54
  562.8 13.4 %all-gather.3 = bf16[16,16,256]{2,1,0:T(8,128)(2,1)S(1)} all-gather(bf16[4,16,256]{2,1,0:T(8,128)(2,1)S(1)} %convolution_convert_fusion.1), channel_id=5, replica_groups=mesh['dp'=8,'mp'=4] {'mp'}, dimensions={0}, use_global_device_ids=true | all-gather | bytes 163840 | tf_op jit(solution)/shard_map/all_gather | solution.py:15
  576.3 10.8 %all-gather.9 = bf16[4,4,16]{2,1,0:T(4,128)(2,1)S(1)} all-gather(bf16[1,4,16]{2,1,0:T(4,128)(2,1)S(1)} %bitcast.754), channel_id=4, replica_groups=mesh['dp'=8,'mp'=4] {'mp'}, dimensions={0}, use_global_device_ids=true | all-gather | bytes 640 | tf_op jit(solution)/shard_map/all_gather | solution.py:15
  587.1 7.6 %all-gather.8 = bf16[4,4,16]{2,1,0:T(4,128)(2,1)S(1)} all-gather(bf16[1,4,16]{2,1,0:T(4,128)(2,1)S(1)} %convert_bitcast_fusion.3), channel_id=3, replica_groups=mesh['dp'=8,'mp'=4] {'mp'}, dimensions={0}, use_global_device_ids=true | all-gather | bytes 640 | tf_op jit(solution)/shard_map/all_gather | solution.py:15
  603.3 13.4 %all-gather.7 = bf16[16,16,256]{2,1,0:T(8,128)(2,1)S(1)} all-gather(bf16[4,16,256]{2,1,0:T(8,128)(2,1)S(1)} %convolution_convert_fusion), channel_id=9, replica_groups=mesh['dp'=8,'mp'=4] {'mp'}, dimensions={0}, use_global_device_ids=true | all-gather | bytes 163840 | tf_op jit(solution)/shard_map/all_gather | solution.py:15
  616.7 9.6 %all-gather.11 = bf16[4,4,16]{2,1,0:T(4,128)(2,1)S(1)} all-gather(bf16[1,4,16]{2,1,0:T(4,128)(2,1)S(1)} %bitcast.753), channel_id=8, replica_groups=mesh['dp'=8,'mp'=4] {'mp'}, dimensions={0}, use_global_device_ids=true | all-gather | bytes 640 | tf_op jit(solution)/shard_map/all_gather | solution.py:15
  626.3 7.6 %all-gather.10 = bf16[4,4,16]{2,1,0:T(4,128)(2,1)S(1)} all-gather(bf16[1,4,16]{2,1,0:T(4,128)(2,1)S(1)} %convert_bitcast_fusion.1), channel_id=7, replica_groups=mesh['dp'=8,'mp'=4] {'mp'}, dimensions={0}, use_global_device_ids=true | all-gather | bytes 640 | tf_op jit(solution)/shard_map/all_gather | solution.py:15
  650.2 51.3 %all-reduce.25.cloned.1.call-done = (f32[32,1024]{1,0:T(8,128)}, f32[32,1024]{1,0:T(8,128)}) async-done(((f32[32,1024]{1,0:T(8,128)}, f32[32,1024]{1,0:T(8,128)}), (f32[32,1024]{1,0:T(8,128)}, f32[32,1024]{1,0:T(8,128)})) %all-reduce.25.cloned.1.call-update) | async-done | bytes 262160
  (329 shorter events, 187.8 us)
Async XLA Ops:
  7.2 553.5 %copy-start = (bf16[4,512,256]{2,1,0:T(8,128)(2,1)S(1)}, bf16[4,512,256]{2,1,0:T(8,128)(2,1)}, u32[]{:S(2)}) copy-start(bf16[4,512,256]{2,1,0:T(8,128)(2,1)} %param.45) | copy-start | bytes 3145732
  42.3 20.3 %all-to-all-start = ((bf16[8,4,512]{2,1,0:T(4,128)(2,1)}), bf16[8,4,512]{2,1,0:T(4,128)(2,1)S(1)}, u32[]{:S(2)}, u32[]{:S(2)}) async-start(bf16[8,4,512]{2,1,0:T(4,128)(2,1)} %constant_dynamic-update-slice_fusion), calls=%async_computation | async-start | bytes 65536 | tf_op jit(solution)/shard_map/all_to_all | solution.py:39
  52.9 103.3 %copy-start.12 = (f32[1,1024]{1,0:T(1,128)}, f32[1,1024]{1,0:T(1,128)S(1)}, u32[]{:S(2)}) copy-start(f32[1,1024]{1,0:T(1,128)S(1)} %get-tuple-element.453) | copy-start | bytes 12292
  54.3 102.0 %copy-start.14 = (f32[1,1024]{1,0:T(1,128)}, f32[1,1024]{1,0:T(1,128)S(1)}, u32[]{:S(2)}) copy-start(f32[1,1024]{1,0:T(1,128)S(1)} %get-tuple-element.447) | copy-start | bytes 12292
  55.7 100.6 %copy-start.16 = (f32[1,1024]{1,0:T(1,128)}, f32[1,1024]{1,0:T(1,128)S(1)}, u32[]{:S(2)}) copy-start(f32[1,1024]{1,0:T(1,128)S(1)} %get-tuple-element.449) | copy-start | bytes 12292
  57.1 99.2 %copy-start.18 = (f32[1,1024]{1,0:T(1,128)}, f32[1,1024]{1,0:T(1,128)S(1)}, u32[]{:S(2)}) copy-start(f32[1,1024]{1,0:T(1,128)S(1)} %get-tuple-element.451) | copy-start | bytes 12292
  62.6 9.1 %all-to-all-start.6 = ((bf16[8,4,512]{2,1,0:T(4,128)(2,1)}), bf16[8,4,512]{2,1,0:T(4,128)(2,1)S(1)}, u32[]{:S(2)}, u32[]{:S(2)}) async-start(bf16[8,4,512]{2,1,0:T(4,128)(2,1)} %constant_dynamic-update-slice_fusion.50), calls=%async_computation.6 | async-start | bytes 65536 | tf_op jit(solution)/shard_map/all_to_all | solution.py:39
  66.8 60.2 %all-reduce.33.cloned.1.call-start = ((), (), s32[]{:S(2)}) async-start(), calls=%async_computation.16 | async-start | bytes 1048576
  72.9 106.4 %copy-start.1 = (bf16[2,512,1024]{2,1,0:T(8,128)(2,1)S(1)}, bf16[2,512,1024]{2,1,0:T(8,128)(2,1)}, u32[]{:S(2)}) copy-start(bf16[2,512,1024]{2,1,0:T(8,128)(2,1)} %param.37) | copy-start | bytes 6291460
  152.9 22.1 %all-to-all-start.1 = ((bf16[8,4,512]{2,1,0:T(4,128)(2,1)}), bf16[8,4,512]{2,1,0:T(4,128)(2,1)S(1)}, u32[]{:S(2)}, u32[]{:S(2)}) async-start(bf16[8,4,512]{2,1,0:T(4,128)(2,1)} %constant_dynamic-update-slice_fusion.8), calls=%async_computation.1 | async-start | bytes 65536 | tf_op jit(solution)/shard_map/all_to_all | solution.py:39
  175.1 9.0 %all-to-all-start.7 = ((bf16[8,4,512]{2,1,0:T(4,128)(2,1)}), bf16[8,4,512]{2,1,0:T(4,128)(2,1)S(1)}, u32[]{:S(2)}, u32[]{:S(2)}) async-start(bf16[8,4,512]{2,1,0:T(4,128)(2,1)} %constant_dynamic-update-slice_fusion.58), calls=%async_computation.7 | async-start | bytes 65536 | tf_op jit(solution)/shard_map/all_to_all | solution.py:39
  179.2 59.3 %all-reduce.31.cloned.1.call-start = ((), (), s32[]{:S(2)}) async-start(), calls=%async_computation.15 | async-start | bytes 524288
  270.9 8.1 %all-to-all-start.2 = ((bf16[8,4,512]{2,1,0:T(4,128)(2,1)}), bf16[8,4,512]{2,1,0:T(4,128)(2,1)S(1)}, u32[]{:S(2)}, u32[]{:S(2)}) async-start(bf16[8,4,512]{2,1,0:T(4,128)(2,1)} %constant_dynamic-update-slice_fusion.16), calls=%async_computation.2 | async-start | bytes 65536 | tf_op jit(solution)/shard_map/all_to_all | solution.py:39
  279.0 9.0 %all-to-all-start.8 = ((bf16[8,4,512]{2,1,0:T(4,128)(2,1)}), bf16[8,4,512]{2,1,0:T(4,128)(2,1)S(1)}, u32[]{:S(2)}, u32[]{:S(2)}) async-start(bf16[8,4,512]{2,1,0:T(4,128)(2,1)} %constant_dynamic-update-slice_fusion.66), calls=%async_computation.8 | async-start | bytes 65536 | tf_op jit(solution)/shard_map/all_to_all | solution.py:39
  283.1 62.8 %all-reduce.29.cloned.1.call-start = ((), (), s32[]{:S(2)}) async-start(), calls=%async_computation.14 | async-start | bytes 1048576
  350.4 135.0 %copy-start.22 = (f32[4096]{0:T(1024)S(1)}, f32[4096]{0:T(1024)}, u32[]{:S(2)}) copy-start(f32[4096]{0:T(1024)} %param.41) | copy-start | bytes 49156
  369.8 22.9 %all-to-all-start.3 = ((bf16[8,4,512]{2,1,0:T(4,128)(2,1)}), bf16[8,4,512]{2,1,0:T(4,128)(2,1)S(1)}, u32[]{:S(2)}, u32[]{:S(2)}) async-start(bf16[8,4,512]{2,1,0:T(4,128)(2,1)} %constant_dynamic-update-slice_fusion.24), calls=%async_computation.3 | async-start | bytes 65536 | tf_op jit(solution)/shard_map/all_to_all | solution.py:39
  392.7 9.0 %all-to-all-start.9 = ((bf16[8,4,512]{2,1,0:T(4,128)(2,1)}), bf16[8,4,512]{2,1,0:T(4,128)(2,1)S(1)}, u32[]{:S(2)}, u32[]{:S(2)}) async-start(bf16[8,4,512]{2,1,0:T(4,128)(2,1)} %constant_dynamic-update-slice_fusion.74), calls=%async_computation.9 | async-start | bytes 65536 | tf_op jit(solution)/shard_map/all_to_all | solution.py:39
  396.9 60.3 %all-reduce.27.cloned.1.call-start = ((), (), s32[]{:S(2)}) async-start(), calls=%async_computation.13 | async-start | bytes 524288
  490.2 8.1 %all-to-all-start.4 = ((bf16[8,4,512]{2,1,0:T(4,128)(2,1)}), bf16[8,4,512]{2,1,0:T(4,128)(2,1)S(1)}, u32[]{:S(2)}, u32[]{:S(2)}) async-start(bf16[8,4,512]{2,1,0:T(4,128)(2,1)} %constant_dynamic-update-slice_fusion.32), calls=%async_computation.4 | async-start | bytes 65536 | tf_op jit(solution)/shard_map/all_to_all | solution.py:39
  498.3 8.9 %all-to-all-start.10 = ((bf16[8,4,512]{2,1,0:T(4,128)(2,1)}), bf16[8,4,512]{2,1,0:T(4,128)(2,1)S(1)}, u32[]{:S(2)}, u32[]{:S(2)}) async-start(bf16[8,4,512]{2,1,0:T(4,128)(2,1)} %constant_dynamic-update-slice_fusion.82), calls=%async_computation.10 | async-start | bytes 65536 | tf_op jit(solution)/shard_map/all_to_all | solution.py:39
  599.9 39.6 %all-to-all-start.5 = ((bf16[8,4,512]{2,1,0:T(4,128)(2,1)}), bf16[8,4,512]{2,1,0:T(4,128)(2,1)S(1)}, u32[]{:S(2)}, u32[]{:S(2)}) async-start(bf16[8,4,512]{2,1,0:T(4,128)(2,1)} %constant_dynamic-update-slice_fusion.42), calls=%async_computation.5 | async-start | bytes 65536 | tf_op jit(solution)/shard_map/all_to_all | solution.py:39
  639.5 9.1 %all-to-all-start.11 = ((bf16[8,4,512]{2,1,0:T(4,128)(2,1)}), bf16[8,4,512]{2,1,0:T(4,128)(2,1)S(1)}, u32[]{:S(2)}, u32[]{:S(2)}) async-start(bf16[8,4,512]{2,1,0:T(4,128)(2,1)} %constant_dynamic-update-slice_fusion.90), calls=%async_computation.11 | async-start | bytes 65536 | tf_op jit(solution)/shard_map/all_to_all | solution.py:39
  643.7 57.8 %all-reduce.25.cloned.1.call-start = ((), (), s32[]{:S(2)}) async-start(), calls=%async_computation.12 | async-start | bytes 524288
  (18 other events, 819.9 us)
Sparse Core Ops, SparseCore 0:
  73.0 54.0 all-reduce.32
  185.1 53.3 all-reduce.30
  291.5 54.3 all-reduce.28
  404.0 53.0 all-reduce.26
  649.7 51.7 all-reduce.24
